TPU v7x, 256 devices: a whole 4x4x8 slice. The times are simulated.
256 devices in a mesh: hot: 64 (over z, y, x_lo), cold: 4 (over x_hi, core).
Axes of the slice: x: 4 (x_hi: 2, x_lo: 2; x = x_hi * 2 + x_lo), y: 4, z: 8, core: 2. Of those that a mesh axis runs over, the one named last changes fastest.
Arguments:
- tokens: bfloat16 [64, 8192], replicated, may hold values from -6 to 6
- norm_gain: float32 [8192], replicated, may hold values from 0.1 to 1.9
- hot_gate: bfloat16 [4096, 8192], P(('hot', 'cold')), may hold values from -0.0625 to 0.0625
- hot_up: bfloat16 [4096, 8192], P(('hot', 'cold')), may hold values from -0.0625 to 0.0625
- hot_down: bfloat16 [4096, 8192], P(('hot', 'cold')), may hold values from -0.21875 to 0.21875
- hot_index: int32 [4096], replicated, may hold values from 0 to 14335, as said below
- cold_gate: bfloat16 [8192, 14336], P('hot', 'cold'), may hold values from -0.0625 to 0.0625
- cold_up: bfloat16 [8192, 14336], P('hot', 'cold'), may hold values from -0.0625 to 0.0625
- cold_down: bfloat16 [14336, 8192], P('cold', 'hot'), may hold values from -0.125 to 0.125
- block_mask: int32 [64, 112], P(None, 'cold'), may hold values from 0 to 1, as said below
Outputs:
- ffn_out: bfloat16 [64, 8192], P(None, ('hot', 'cold'))
Inputs may be any that keep to these rules, and one draw needn't show every extreme that they name: `hot_index`: distinct hidden units. `block_mask`: in each run of 28 blocks held by one index of cold, at most 14 blocks are active for any sequence, and some index reaches exactly 14.
All inputs are finite; a program needn't handle non-finite values.
Results may differ from a plain program's by a relative error of at most 0.0065.
Values may be sent and summed in bfloat16 or wider, within the bound.
A program may use at most 64 MiB of HBM per device.

v0:
```python
import jax
import jax.numpy as jnp
from jax import lax
from jax.sharding import Mesh
from jax.sharding import PartitionSpec as P

UNITS = 14336
COLD = ("cold_0", "cold_1")
HOT = ("hot_0", "hot_1", "hot_2")
HOT_COLD = ("hot_0", "hot_1", "hot_2", "cold_0", "cold_1")


def copy_for_each(x, axis):
    devices = lax.axis_size(axis)
    return lax.all_to_all(jnp.broadcast_to(x[None], (devices, *x.shape)), axis, 0, 0, tiled=True)


def joined_along(pieces, dim):
    shape = list(pieces.shape[1:])
    shape[dim] *= pieces.shape[0]
    return jnp.moveaxis(pieces, 0, dim).reshape(shape)


def collect(x, axis, dim):
    pieces = copy_for_each(x, axis)
    return joined_along(pieces, dim)


def all_blocks(x, axes, sequence):
    pieces = x
    for k in sequence:
        pieces = lax.all_gather(pieces, axes[k])
    done = sequence[::-1]
    back = [done.index(k) for k in range(len(axes))]
    pieces = pieces.transpose(*back, *range(len(axes), pieces.ndim))
    return pieces.reshape(-1, *x.shape)


def gathered_by_axis(x, axes, sequence, dim):
    return joined_along(all_blocks(x, axes, sequence), dim)


def cut_along(x, dim, devices):
    before, after = (x.shape[:dim], x.shape[dim + 1 :])
    return jnp.moveaxis(x.reshape(*before, devices, -1, *after), dim, 0)


def summed_on_arrival(x, axis, dim):
    pieces = cut_along(x, dim, lax.axis_size(axis))
    arrived = lax.all_to_all(pieces, axis, split_axis=0, concat_axis=0, tiled=True)
    return arrived.sum(axis=0)


def on_device(
    tokens,
    norm_gain,
    hot_gate,
    hot_up,
    hot_down,
    hot_index,
    cold_gate,
    cold_up,
    cold_down,
    block_mask,
):
    values = tokens.astype(jnp.float32)
    scale = lax.rsqrt(jnp.mean(values * values, axis=1, keepdims=True) + 1e-05)
    normed = (values * scale * norm_gain[None, :]).astype(jnp.bfloat16)
    dims = (((1,), (1,)), ((), ()))
    gate_hot = lax.dot_general(normed, hot_gate, dims, preferred_element_type=jnp.float32)
    up_hot = lax.dot_general(normed, hot_up, dims, preferred_element_type=jnp.float32)
    hidden_hot = (jax.nn.silu(gate_hot) * up_hot).astype(jnp.bfloat16)
    feat_rows = cold_gate.shape[0]
    unit_count = cold_gate.shape[1]
    out_cols = cold_down.shape[1]
    blocks_here = block_mask.shape[1]
    block = unit_count // blocks_here
    seqs = tokens.shape[0]
    is_hot = jnp.zeros((UNITS,), jnp.float32).at[hot_index].set(1.0)
    local_hot = lax.dynamic_slice_in_dim(is_hot, lax.axis_index(COLD) * unit_count, unit_count)
    capacity = blocks_here // 2
    positions = jnp.arange(blocks_here, dtype=jnp.int32)
    active = jnp.max(block_mask, axis=0) > 0
    slots = jnp.argsort(jnp.where(active, positions, positions + blocks_here))[:capacity]
    gate_w = cold_gate.reshape(feat_rows, blocks_here, block)[:, slots].reshape(
        feat_rows, capacity * block
    )
    up_w = cold_up.reshape(feat_rows, blocks_here, block)[:, slots].reshape(
        feat_rows, capacity * block
    )
    down_w = cold_down.reshape(blocks_here, block, out_cols)[slots].reshape(
        capacity * block, out_cols
    )
    seq_live = block_mask[:, slots].astype(jnp.float32)
    unit_live = 1.0 - local_hot.reshape(blocks_here, block)[slots]
    live = (seq_live[:, :, None] * unit_live[None, :, :]).reshape(seqs, capacity * block)
    gate_cols, up_cols = (
        lax.all_to_all(gate_w, HOT, split_axis=1, concat_axis=0, tiled=True),
        lax.all_to_all(up_w, HOT, split_axis=1, concat_axis=0, tiled=True),
    )
    gate_share = jnp.dot(normed, gate_cols, preferred_element_type=jnp.float32)
    up_share = jnp.dot(normed, up_cols, preferred_element_type=jnp.float32)
    share = gate_share.shape[1]
    live_share = lax.dynamic_slice_in_dim(live, lax.axis_index(HOT) * share, share, 1)
    piece = (jax.nn.silu(gate_share) * up_share * live_share).astype(jnp.bfloat16)
    hidden_cold = collect(piece, HOT, 1)
    out_cold = jnp.dot(hidden_cold, down_w, preferred_element_type=jnp.float32)
    down_cols = lax.all_to_all(hot_down, HOT_COLD, split_axis=1, concat_axis=0, tiled=True)
    hidden_all = gathered_by_axis(
        hidden_hot, (("hot_0", "hot_1", "hot_2", "cold_0"), "cold_1"), (0, 1), 1
    )
    hot_total = jnp.dot(hidden_all, down_cols, preferred_element_type=jnp.float32)
    cold_total = summed_on_arrival(out_cold, COLD, 1)
    total = hot_total + cold_total
    return total.astype(jnp.bfloat16)


def solution(mesh):
    split = Mesh(
        mesh.devices.reshape(8, 4, 2, 2, 2), ("hot_0", "hot_1", "hot_2", "cold_0", "cold_1")
    )
    placed = (
        P(),
        P(),
        P(HOT_COLD, None),
        P(HOT_COLD, None),
        P(HOT_COLD, None),
        P(),
        P(HOT, COLD),
        P(HOT, COLD),
        P(COLD, HOT),
        P(None, COLD),
    )
    return jax.shard_map(
        on_device, mesh=split, in_specs=placed, out_specs=P(None, HOT_COLD), check_vma=False
    )
```

profile of v0, /device:TPU:1, one launch (start us, length us, event | category | flops | bytes accessed | tf_op | source)
XLA Modules:
  0.0 460.4 jit_solution(4958017223762994111)
XLA Ops:
  0.0 0.9 reduce_max.9
  0.9 1.6 sort.17
  2.6 1.6 copy.32
  4.1 0.6 copy.33
  4.8 0.6 gather_fusion
  5.7 0.9 all_to_all.49
  6.6 13.6 %all-to-all-start.1 = ((bf16[128,64,28]{0,2,1:T(8,128)(2,1)}), bf16[128,64,28]{0,2,1:T(8,128)(2,1)S(1)}, u32[]{:S(2)}, u32[]{:S(2)}) async-start(bf16[128,64,28]{0,2,1:T(8,128)(2,1)} %all_to_all.49), calls=%async_computation.1 | async-start | bytes 1048576 | tf_op jit(solution)/shard_map/all_to_all | solution.py:98
  20.2 0.6 copy.36
  20.8 0.6 copy.37
  21.5 0.6 gather_fusion.1
  22.4 0.9 all_to_all.53
  23.3 15.5 %scatter_custom_fusion = f32[14336]{0:T(1024)S(1)} fusion(s32[4096]{0:T(1024)S(1)} %compare_select_fusion, f32[4096]{0:T(1024)S(1)} %broadcast.41, f32[]{:T(128)} %constant.17.clone.1), kind=kCustom, calls=%fused_computation.27 | custom fusion | bytes 57348 | tf_op jit(solution)/shard_map/scatter | solution.py:79
  38.9 10.9 %all-to-all-start.2 = ((bf16[128,64,28]{0,2,1:T(8,128)(2,1)}), bf16[128,64,28]{0,2,1:T(8,128)(2,1)}, u32[]{:S(2)}, u32[]{:S(2)}) async-start(bf16[128,64,28]{0,2,1:T(8,128)(2,1)} %all_to_all.53), calls=%async_computation.2 | async-start | bytes 1048576 | tf_op jit(solution)/shard_map/all_to_all | solution.py:99
  49.9 0.6 gather_fusion.2
  50.5 0.6 gather_fusion.3
  51.0 0.8 all_to_all.46
  51.8 0.7 copy.51
  52.5 1.4 reshape.134
  54.0 0.3 fusion
  54.6 0.3 copy.44
  54.9 9.8 %all-to-all-done.2 = bf16[128,64,28]{0,2,1:T(8,128)(2,1)} async-done(((bf16[128,64,28]{0,2,1:T(8,128)(2,1)}), bf16[128,64,28]{0,2,1:T(8,128)(2,1)}, u32[]{:S(2)}, u32[]{:S(2)}) %all-to-all-start.2) | async-done | bytes 458784 | tf_op jit(solution)/shard_map/all_to_all | solution.py:99
  64.7 1.2 copy.49
  66.0 0.3 copy.45
  66.4 0.3 copy-done.9
  66.7 0.5 fusion.15
  67.3 0.5 fusion.6
  67.8 1.0 reshape.130
  68.8 7.0 %all-to-all-start.3 = ((bf16[64,2,896]{2,1,0:T(2,128)(2,1)}), bf16[64,2,896]{2,1,0:T(2,128)(2,1)S(1)}, u32[]{:S(2)}, u32[]{:S(2)}) async-start(bf16[64,2,896]{2,1,0:T(2,128)(2,1)} %reshape.130), calls=%async_computation.3 | async-start | bytes 458752 | tf_op jit(solution)/shard_map/all_to_all | solution.py:15
  75.8 0.5 fusion.18
  76.2 0.5 copy-done.8
  76.7 0.5 fusion.8
  77.2 8.9 %all-to-all-done.3 = bf16[64,2,896]{2,1,0:T(2,128)(2,1)S(1)} async-done(((bf16[64,2,896]{2,1,0:T(2,128)(2,1)}), bf16[64,2,896]{2,1,0:T(2,128)(2,1)S(1)}, u32[]{:S(2)}, u32[]{:S(2)}) %all-to-all-start.3) | async-done | bytes 229408 | tf_op jit(solution)/shard_map/all_to_all | solution.py:15
  86.1 10.0 %all-to-all-start = ((bf16[256,2,256]{2,1,0:T(2,128)(2,1)}), bf16[256,2,256]{2,1,0:T(2,128)(2,1)S(1)}, u32[]{:S(2)}, u32[]{:S(2)}) async-start(bf16[256,2,256]{2,1,0:T(2,128)(2,1)} %reshape.134), calls=%async_computation | async-start | bytes 524288 | tf_op jit(solution)/shard_map/all_to_all | solution.py:108
  96.1 294.4 %all-gather.2 = bf16[128,64,16]{1,2,0:T(8,128)(2,1)S(1)} all-gather(bf16[1,64,16]{1,2,0:T(8,128)(2,1)S(1)} %fusion.8), channel_id=2, replica_groups=mesh['hot_0'=8,'hot_1'=4,'hot_2'=2,'cold_0'=2,'cold_1'=2] {'hot_0','hot_..., dimensions={0}, use_global_device_ids=true | all-gather | bytes 264192 | tf_op jit(solution)/shard_map/all_gather | solution.py:32
  390.5 0.8 gather_fusion.4
  391.5 0.6 copy.27
  392.1 0.3 reshape.131
  392.6 0.3 fusion.20
  392.9 0.7 reshape.132
  393.6 58.8 %all-to-all-start.4 = ((f32[4,1,2048]{2,1,0:T(1,128)}), f32[4,1,2048]{2,1,0:T(1,128)S(1)}, u32[]{:S(2)}, u32[]{:S(2)}) async-start(f32[4,1,2048]{2,1,0:T(1,128)} %reshape.132), calls=%async_computation.4 | async-start | bytes 65536 | tf_op jit(solution)/shard_map/all_to_all | solution.py:50
  452.4 2.2 all-gather.1
  454.8 1.2 copy.28
  456.0 0.8 copy.29
  456.9 0.5 reshape.135
  457.4 0.8 copy.31
  458.2 0.5 broadcast.58
  458.7 0.7 reduce
  459.6 0.9 fusion.5
  (45 shorter events, 1.9 us)
Async XLA Ops:
  0.0 390.5 %copy-start = (bf16[3584,128]{1,0:T(8,128)(2,1)S(1)}, bf16[3584,128]{1,0:T(8,128)(2,1)}, u32[]{:S(2)}) copy-start(bf16[3584,128]{1,0:T(8,128)(2,1)} %param.18) | copy-start | bytes 2752516
  2.6 47.9 %copy-start.6 = (s32[1024]{0:T(1024)}, s32[1024]{0:T(1024)S(1)}, u32[]{:S(2)}) copy-start(s32[1024]{0:T(1024)S(1)} %pad_clamp_fusion) | copy-start | bytes 12292
  5.7 14.5 %copy-start.3 = (bf16[128,3584]{1,0:T(8,128)(2,1)S(1)}, bf16[128,3584]{1,0:T(8,128)(2,1)}, u32[]{:S(2)}) copy-start(bf16[128,3584]{1,0:T(8,128)(2,1)} %param.17) | copy-start | bytes 2752516
  6.6 32.3 %all-to-all-start.1 = ((bf16[128,64,28]{0,2,1:T(8,128)(2,1)}), bf16[128,64,28]{0,2,1:T(8,128)(2,1)S(1)}, u32[]{:S(2)}, u32[]{:S(2)}) async-start(bf16[128,64,28]{0,2,1:T(8,128)(2,1)} %all_to_all.49), calls=%async_computation.1 | async-start | bytes 1048576 | tf_op jit(solution)/shard_map/all_to_all | solution.py:98
  22.1 1.2 copy-start.5
  22.4 27.5 %copy-start.1 = (s32[64,28]{0,1:T(8,128)S(1)}, s32[64,28]{0,1:T(8,128)}, u32[]{:S(2)}) copy-start(s32[64,28]{0,1:T(8,128)} %param.19) | copy-start | bytes 21508
  22.4 28.6 %copy-start.4 = (bf16[16,8192]{1,0:T(8,128)(2,1)S(1)}, bf16[16,8192]{1,0:T(8,128)(2,1)}, u32[]{:S(2)}) copy-start(bf16[16,8192]{1,0:T(8,128)(2,1)} %param.14) | copy-start | bytes 786436
  38.9 25.9 %all-to-all-start.2 = ((bf16[128,64,28]{0,2,1:T(8,128)(2,1)}), bf16[128,64,28]{0,2,1:T(8,128)(2,1)}, u32[]{:S(2)}, u32[]{:S(2)}) async-start(bf16[128,64,28]{0,2,1:T(8,128)(2,1)} %all_to_all.53), calls=%async_computation.2 | async-start | bytes 1048576 | tf_op jit(solution)/shard_map/all_to_all | solution.py:99
  52.5 1.5 copy-start.2
  65.9 0.8 copy-start.9
  67.7 8.0 %copy-start.7 = (bf16[16,8192]{1,0:T(8,128)(2,1)S(1)}, bf16[16,8192]{1,0:T(8,128)(2,1)}, u32[]{:S(2)}) copy-start(bf16[16,8192]{1,0:T(8,128)(2,1)} %param.12) | copy-start | bytes 786436
  68.8 17.3 %all-to-all-start.3 = ((bf16[64,2,896]{2,1,0:T(2,128)(2,1)}), bf16[64,2,896]{2,1,0:T(2,128)(2,1)S(1)}, u32[]{:S(2)}, u32[]{:S(2)}) async-start(bf16[64,2,896]{2,1,0:T(2,128)(2,1)} %reshape.130), calls=%async_computation.3 | async-start | bytes 458752 | tf_op jit(solution)/shard_map/all_to_all | solution.py:15
  75.8 1.0 copy-start.8
  86.1 307.5 %all-to-all-start = ((bf16[256,2,256]{2,1,0:T(2,128)(2,1)}), bf16[256,2,256]{2,1,0:T(2,128)(2,1)S(1)}, u32[]{:S(2)}, u32[]{:S(2)}) async-start(bf16[256,2,256]{2,1,0:T(2,128)(2,1)} %reshape.134), calls=%async_computation | async-start | bytes 524288 | tf_op jit(solution)/shard_map/all_to_all | solution.py:108
  393.6 64.6 %all-to-all-start.4 = ((f32[4,1,2048]{2,1,0:T(1,128)}), f32[4,1,2048]{2,1,0:T(1,128)S(1)}, u32[]{:S(2)}, u32[]{:S(2)}) async-start(f32[4,1,2048]{2,1,0:T(1,128)} %reshape.132), calls=%async_computation.4 | async-start | bytes 65536 | tf_op jit(solution)/shard_map/all_to_all | solution.py:50
where the time goes:
time: 461 us; the launch traced here: 460 us
  blocking collectives  297 us (64%)
  starting transfers between devices  100 us (22%)
  local copies, waits for them, and re-layouts  37.9 us (8%)
  waiting for transfers between devices  18.7 us (4%)
    all_gather x2, blocking collectives, all_blocks(): pieces = lax.all_gather(pieces, axes[k])  297 us
    all_to_all x1, starting transfers between devices, summed_on_arrival(): lax.all_to_all(pieces, axis, split_axis=0, concat_axis=0, tiled=True)  58.8 us
    scatter x1, local copies, waits for them, and re-layouts, on_device(): is_hot = jnp.zeros((UNITS,), jnp.float32).at[hot_index].set(1.0)  15.5 us
    all_to_all x1, starting transfers between devices, on_device(): lax.all_to_all(gate_w, HOT, split_axis=1, concat_axis=0, tiled=True)  13.6 us
    all_to_all x1, starting transfers between devices, on_device(): lax.all_to_all(up_w, HOT, split_axis=1, concat_axis=0, tiled=True)  10.9 us
    all_to_all x1, starting transfers between devices, on_device(): lax.all_to_all(hot_down, HOT_COLD, split_axis=1, concat_axis=0, tiled=True)  9.98 us
    all_to_all x1, waiting for transfers between devices, on_device(): lax.all_to_all(up_w, HOT, split_axis=1, concat_axis=0, tiled=True)  9.79 us
  transfers between devices with their start and end apart: 5, of which 2 were waited for; matrix products, arithmetic and copies ran while one was open for 6% of the time, Pallas kernels for 0%

commit v1 on v0

--- a/solution.py
+++ b/solution.py
@@ -105,7 +105,12 @@
     piece = (jax.nn.silu(gate_share) * up_share * live_share).astype(jnp.bfloat16)
     hidden_cold = collect(piece, HOT, 1)
     out_cold = jnp.dot(hidden_cold, down_w, preferred_element_type=jnp.float32)
-    down_cols = lax.all_to_all(hot_down, HOT_COLD, split_axis=1, concat_axis=0, tiled=True)
+    down_cols = jnp.concatenate(
+        lax.all_to_all(
+            jnp.stack(jnp.split(hot_down, lax.axis_size(HOT_COLD), axis=1)), HOT_COLD, 0, 0
+        ),
+        axis=0,
+    )
     hidden_all = gathered_by_axis(
         hidden_hot, (("hot_0", "hot_1", "hot_2", "cold_0"), "cold_1"), (0, 1), 1
     )

time: 461 us -> 625 us (1.36)
  local copies, waits for them, and re-layouts: 37.9 us -> 203 us
    unnamed x33 -> x290, local copies, waits for them, and re-layouts: 7.92 us -> 175 us
  transfers between devices with their start and end apart: 5 -> 5, of which waited for: 2 -> 2; matrix products, arithmetic and copies ran while one was open for 6% -> 31% of each run, Pallas kernels for 0% -> 0%
where the time goes in v1:
time: 625 us
  blocking collectives  297 us (48%)
  local copies, waits for them, and re-layouts  203 us (32%)
  starting transfers between devices  100 us (16%)
  waiting for transfers between devices  17.5 us (3%)
    all_gather x2, blocking collectives, all_blocks(): pieces = lax.all_gather(pieces, axes[k])  297 us
    unnamed x290, local copies, waits for them, and re-layouts  175 us
    all_to_all x1, starting transfers between devices, summed_on_arrival(): lax.all_to_all(pieces, axis, split_axis=0, concat_axis=0, tiled=True)  58.8 us
    scatter x1, local copies, waits for them, and re-layouts, on_device(): is_hot = jnp.zeros((UNITS,), jnp.float32).at[hot_index].set(1.0)  15.5 us
    all_to_all x1, starting transfers between devices, on_device(): lax.all_to_all(gate_w, HOT, split_axis=1, concat_axis=0, tiled=True)  13.6 us
  transfers between devices with their start and end apart: 5, of which 2 were waited for; matrix products, arithmetic and copies ran while one was open for 31% of the time, Pallas kernels for 0%

profile of v1, /device:TPU:1, one launch (start us, length us, event | category | flops | bytes accessed | tf_op | source)
XLA Modules:
  0.0 624.6 jit_solution(11862046659761710514)
XLA Ops:
  0.0 0.9 reduce_max.9
  0.9 1.6 sort.17
  2.6 1.6 copy.571
  5.7 0.9 all_to_all.38
  6.6 13.6 %all-to-all-start.1 = ((bf16[128,64,28]{0,2,1:T(8,128)(2,1)}), bf16[128,64,28]{0,2,1:T(8,128)(2,1)S(1)}, u32[]{:S(2)}, u32[]{:S(2)}) async-start(bf16[128,64,28]{0,2,1:T(8,128)(2,1)} %all_to_all.38), calls=%async_computation.1 | async-start | bytes 1048576 | tf_op jit(solution)/shard_map/all_to_all | solution.py:98
  24.1 0.7 constant_dynamic-update-slice_fusion.249
  26.7 0.7 constant_dynamic-update-slice_fusion.245
  33.8 0.7 constant_dynamic-update-slice_fusion.234
  50.6 0.7 constant_dynamic-update-slice_fusion.208
  57.1 0.7 constant_dynamic-update-slice_fusion.198
  60.3 0.7 constant_dynamic-update-slice_fusion.193
  71.3 0.7 constant_dynamic-update-slice_fusion.176
  75.2 0.7 constant_dynamic-update-slice_fusion.170
  84.3 0.7 constant_dynamic-update-slice_fusion.156
  94.6 0.7 constant_dynamic-update-slice_fusion.140
  107.5 0.7 constant_dynamic-update-slice_fusion.120
  112.7 0.7 constant_dynamic-update-slice_fusion.112
  132.0 0.7 constant_dynamic-update-slice_fusion.82
  142.3 0.7 constant_dynamic-update-slice_fusion.66
  145.6 0.7 constant_dynamic-update-slice_fusion.61
  161.1 0.7 constant_dynamic-update-slice_fusion.37
  169.5 0.7 constant_dynamic-update-slice_fusion.24
  174.0 0.7 constant_dynamic-update-slice_fusion.17
  176.6 0.7 constant_dynamic-update-slice_fusion.13
  179.9 0.7 constant_dynamic-update-slice_fusion.8
  181.1 0.7 constant_dynamic-update-slice_fusion.6
  184.4 0.8 gather_fusion.1
  185.4 0.9 all_to_all.42
  186.3 15.5 %scatter_custom_fusion = f32[14336]{0:T(1024)S(1)} fusion(s32[4096]{0:T(1024)S(1)} %compare_select_fusion, f32[4096]{0:T(1024)S(1)} %broadcast.41, f32[]{:T(128)} %constant.17.clone.1), kind=kCustom, calls=%fused_computation.283 | custom fusion | bytes 57348 | tf_op jit(solution)/shard_map/scatter | solution.py:79
  204.5 10.8 %all-to-all-start.2 = ((bf16[128,64,28]{0,2,1:T(8,128)(2,1)}), bf16[128,64,28]{0,2,1:T(8,128)(2,1)S(1)}, u32[]{:S(2)}, u32[]{:S(2)}) async-start(bf16[128,64,28]{0,2,1:T(8,128)(2,1)} %all_to_all.42), calls=%async_computation.2 | async-start | bytes 1048576 | tf_op jit(solution)/shard_map/all_to_all | solution.py:99
  215.4 0.8 gather_fusion.2
  216.2 0.7 gather_fusion.3
  216.9 2.9 reshape.132
  220.5 1.1 copy.583
  221.6 8.6 %all-to-all-done.2 = bf16[128,64,28]{0,2,1:T(8,128)(2,1)S(1)} async-done(((bf16[128,64,28]{0,2,1:T(8,128)(2,1)}), bf16[128,64,28]{0,2,1:T(8,128)(2,1)S(1)}, u32[]{:S(2)}, u32[]{:S(2)}) %all-to-all-start.2) | async-done | bytes 458784 | tf_op jit(solution)/shard_map/all_to_all | solution.py:99
  232.6 1.0 reshape.128
  233.6 7.0 %all-to-all-start.3 = ((bf16[64,2,896]{2,1,0:T(2,128)(2,1)}), bf16[64,2,896]{2,1,0:T(2,128)(2,1)S(1)}, u32[]{:S(2)}, u32[]{:S(2)}) async-start(bf16[64,2,896]{2,1,0:T(2,128)(2,1)} %reshape.128), calls=%async_computation.3 | async-start | bytes 458752 | tf_op jit(solution)/shard_map/all_to_all | solution.py:15
  242.0 8.9 %all-to-all-done.3 = bf16[64,2,896]{2,1,0:T(2,128)(2,1)S(1)} async-done(((bf16[64,2,896]{2,1,0:T(2,128)(2,1)}), bf16[64,2,896]{2,1,0:T(2,128)(2,1)S(1)}, u32[]{:S(2)}, u32[]{:S(2)}) %all-to-all-start.3) | async-done | bytes 229408 | tf_op jit(solution)/shard_map/all_to_all | solution.py:15
  250.9 10.0 %all-to-all-start = ((bf16[256,2,256]{2,1,0:T(2,128)(2,1)}), bf16[256,2,256]{2,1,0:T(2,128)(2,1)S(1)}, u32[]{:S(2)}, u32[]{:S(2)}) async-start(bf16[256,2,256]{2,1,0:T(2,128)(2,1)} %reshape.132), calls=%async_computation | async-start | bytes 524288 | tf_op jit(solution)/shard_map/all_to_all | solution.py:109
  260.8 294.4 %all-gather.2 = bf16[128,64,16]{1,2,0:T(8,128)(2,1)S(1)} all-gather(bf16[1,64,16]{1,2,0:T(8,128)(2,1)S(1)} %fusion.8), channel_id=2, replica_groups=mesh['hot_0'=8,'hot_1'=4,'hot_2'=2,'cold_0'=2,'cold_1'=2] {'hot_0','hot_..., dimensions={0}, use_global_device_ids=true | all-gather | bytes 264192 | tf_op jit(solution)/shard_map/all_gather | solution.py:32
  555.3 0.8 gather_fusion.4
  557.7 0.7 reshape.130
  558.4 58.8 %all-to-all-start.4 = ((f32[4,1,2048]{2,1,0:T(1,128)}), f32[4,1,2048]{2,1,0:T(1,128)S(1)}, u32[]{:S(2)}, u32[]{:S(2)}) async-start(f32[4,1,2048]{2,1,0:T(1,128)} %reshape.130), calls=%async_computation.4 | async-start | bytes 65536 | tf_op jit(solution)/shard_map/all_to_all | solution.py:50
  617.2 2.2 all-gather.1
  619.5 1.2 copy.568
  620.8 0.8 copy.569
  622.7 0.7 reduce
  623.5 1.1 fusion.5
  (300 shorter events, 161.7 us)
Async XLA Ops:
  0.0 555.3 %copy-start = (bf16[3584,128]{1,0:T(8,128)(2,1)S(1)}, bf16[3584,128]{1,0:T(8,128)(2,1)}, u32[]{:S(2)}) copy-start(bf16[3584,128]{1,0:T(8,128)(2,1)} %param.18) | copy-start | bytes 2752516
  2.6 4.1 copy-start.7
  5.7 14.5 %copy-start.6 = (s32[4096]{0:T(1024)S(1)}, s32[4096]{0:T(1024)}, u32[]{:S(2)}) copy-start(s32[4096]{0:T(1024)} %param.15) | copy-start | bytes 49156
  5.7 14.5 %copy-start.2 = (bf16[16,8192]{1,0:T(8,128)(2,1)S(1)}, bf16[16,8192]{1,0:T(8,128)(2,1)}, u32[]{:S(2)}) copy-start(bf16[16,8192]{1,0:T(8,128)(2,1)} %param.14) | copy-start | bytes 786436
  6.6 197.9 %all-to-all-start.1 = ((bf16[128,64,28]{0,2,1:T(8,128)(2,1)}), bf16[128,64,28]{0,2,1:T(8,128)(2,1)S(1)}, u32[]{:S(2)}, u32[]{:S(2)}) async-start(bf16[128,64,28]{0,2,1:T(8,128)(2,1)} %all_to_all.38), calls=%async_computation.1 | async-start | bytes 1048576 | tf_op jit(solution)/shard_map/all_to_all | solution.py:98
  20.2 162.9 %copy-start.4 = (bf16[128,3584]{1,0:T(8,128)(2,1)S(1)}, bf16[128,3584]{1,0:T(8,128)(2,1)}, u32[]{:S(2)}) copy-start(bf16[128,3584]{1,0:T(8,128)(2,1)} %param.17) | copy-start | bytes 2752516
  185.4 30.0 %copy-start.1 = (s32[64,28]{0,1:T(8,128)S(1)}, s32[64,28]{0,1:T(8,128)}, u32[]{:S(2)}) copy-start(s32[64,28]{0,1:T(8,128)} %param.19) | copy-start | bytes 21508
  204.5 25.7 %all-to-all-start.2 = ((bf16[128,64,28]{0,2,1:T(8,128)(2,1)}), bf16[128,64,28]{0,2,1:T(8,128)(2,1)S(1)}, u32[]{:S(2)}, u32[]{:S(2)}) async-start(bf16[128,64,28]{0,2,1:T(8,128)(2,1)} %all_to_all.42), calls=%async_computation.2 | async-start | bytes 1048576 | tf_op jit(solution)/shard_map/all_to_all | solution.py:99
  215.3 4.6 copy-start.3
  230.4 1.0 copy-start.5
  230.4 1.0 copy-start.10
  232.5 8.0 %copy-start.8 = (bf16[16,8192]{1,0:T(8,128)(2,1)S(1)}, bf16[16,8192]{1,0:T(8,128)(2,1)}, u32[]{:S(2)}) copy-start(bf16[16,8192]{1,0:T(8,128)(2,1)} %param.12) | copy-start | bytes 786436
  233.6 17.3 %all-to-all-start.3 = ((bf16[64,2,896]{2,1,0:T(2,128)(2,1)}), bf16[64,2,896]{2,1,0:T(2,128)(2,1)S(1)}, u32[]{:S(2)}, u32[]{:S(2)}) async-start(bf16[64,2,896]{2,1,0:T(2,128)(2,1)} %reshape.128), calls=%async_computation.3 | async-start | bytes 458752 | tf_op jit(solution)/shard_map/all_to_all | solution.py:15
  240.5 1.0 copy-start.9
  250.9 307.5 %all-to-all-start = ((bf16[256,2,256]{2,1,0:T(2,128)(2,1)}), bf16[256,2,256]{2,1,0:T(2,128)(2,1)S(1)}, u32[]{:S(2)}, u32[]{:S(2)}) async-start(bf16[256,2,256]{2,1,0:T(2,128)(2,1)} %reshape.132), calls=%async_computation | async-start | bytes 524288 | tf_op jit(solution)/shard_map/all_to_all | solution.py:109
  558.4 63.8 %all-to-all-start.4 = ((f32[4,1,2048]{2,1,0:T(1,128)}), f32[4,1,2048]{2,1,0:T(1,128)S(1)}, u32[]{:S(2)}, u32[]{:S(2)}) async-start(f32[4,1,2048]{2,1,0:T(1,128)} %reshape.130), calls=%async_computation.4 | async-start | bytes 65536 | tf_op jit(solution)/shard_map/all_to_all | solution.py:50
